TPU v7x, 32 devices: a whole 2x2x4 slice. The times are simulated.
32 devices in a mesh: gx: 4 (over x, core), gy: 8 (over z, y).
Axes of the slice: x: 2, y: 2, z: 4, core: 2. Of those that a mesh axis runs over, the one named last changes fastest.
Arguments:
- hot_ids: int32 [262144], P(('gx', 'gy')), may hold values from 0 to 2047
- hot_grads: bfloat16 [262144, 128], P(('gx', 'gy')), may hold values from -6 to 6
- cold_grads: bfloat16 [4, 8, 8, 512, 128], P('gx', 'gy'), may hold values from -6 to 6
- cold_slots: int32 [4, 8, 8, 512], P('gx', 'gy'), may hold values from 0 to 2047
- cold_counts: int32 [4, 8, 8], P('gx', 'gy'), may hold values from 1 to 512, as said below
Outputs:
- hot_grad: float32 [2048, 128], replicated
- cold_grad: float32 [4, 16384, 128], P('gx', 'gy')
Inputs may be any that keep to these rules, and one draw needn't show every extreme that they name: In each group g, some owner d receives cold_counts[g, s, d] = 512 from every s; loads per owner are skewed.
All inputs are finite; a program needn't handle non-finite values.
Results may differ from a plain program's by a relative error of at most 0.0003.
Values may be sent and summed in bfloat16 or wider, within the bound.
A program may use at most 64 MiB of HBM per device.

v0:
```python
import math
import jax
import jax.numpy as jnp
from jax import lax
from jax.sharding import PartitionSpec as P

HOT = 2048
OWN_ROWS = 2048


def onehot_sum(row_ids, row_data, table_size, block_rows):
    turns = row_ids.shape[0] // block_rows
    id_blocks = row_ids.reshape(turns, block_rows)
    data_blocks = row_data.reshape(turns, block_rows, row_data.shape[1])
    table_iota = lax.broadcasted_iota(jnp.int32, (table_size, block_rows), 0)

    def add_block(total, pieces):
        ids_here, data_here = pieces
        selector = (table_iota == ids_here[None, :]).astype(jnp.bfloat16)
        return (total + jnp.dot(selector, data_here, preferred_element_type=jnp.float32), None)

    start = jnp.zeros((table_size, row_data.shape[1]), jnp.float32)
    total, unused = lax.scan(add_block, start, (id_blocks, data_blocks))
    return total


def hot_part(hot_ids, hot_grads):
    hot_rows = HOT
    block_rows = math.gcd(hot_ids.shape[0], 2048)
    local_sum = onehot_sum(hot_ids, hot_grads, hot_rows, block_rows)
    factor = (hot_rows / (hot_ids.shape[0] * lax.axis_size("gx") * lax.axis_size("gy"))) ** 0.5
    shared = lax.psum_scatter(local_sum, "gy", scatter_dimension=0, tiled=True)
    shared = lax.psum(shared, "gx")
    total = lax.all_gather(shared, "gy", axis=0, tiled=True)
    return total * factor


def cold_part(cold_grads, cold_slots, cold_counts):
    owners, capacity, width = (cold_grads.shape[2], cold_grads.shape[3], cold_grads.shape[4])
    grads_here = cold_grads.reshape(owners, capacity, width)
    slots_here = cold_slots.reshape(owners, capacity)
    counts_here = cold_counts.reshape(owners)
    places = lax.broadcasted_iota(jnp.int32, (owners, capacity), 1)
    valid = places < counts_here[:, None]
    payload = jnp.where(valid[:, :, None], grads_here, jnp.zeros_like(grads_here))
    got_rows, got_slots = (
        lax.all_to_all(payload, "gy", split_axis=0, concat_axis=0, tiled=True),
        lax.all_to_all(slots_here, "gy", split_axis=0, concat_axis=0, tiled=True),
    )
    total_rows = owners * capacity
    block_rows = math.gcd(total_rows, 1024)
    table = onehot_sum(
        got_slots.reshape(total_rows), got_rows.reshape(total_rows, width), OWN_ROWS, block_rows
    )
    return table.reshape(1, OWN_ROWS, width)


def per_device(hot_ids, hot_grads, cold_grads, cold_slots, cold_counts):
    hot_grad = hot_part(hot_ids, hot_grads)
    cold_grad = cold_part(cold_grads, cold_slots, cold_counts)
    return (hot_grad, cold_grad)


def solution(mesh):
    return jax.shard_map(
        per_device,
        mesh=mesh,
        in_specs=(
            P(("gx", "gy")),
            P(("gx", "gy"), None),
            P("gx", "gy", None, None, None),
            P("gx", "gy", None, None),
            P("gx", "gy", None),
        ),
        out_specs=(P(), P("gx", "gy", None)),
        check_vma=False,
    )
```

profile of v0, /device:TPU:0, one launch (start us, length us, event | category | flops | bytes accessed | tf_op | source)
XLA Modules:
  0.0 185.8 jit_solution(4274179711939193013)
XLA Ops:
  7.2 0.0 reduce-scatter.2.cloned.1.call-start
  7.2 0.8 reshape.43
  8.0 0.0 copy-start.2
  8.0 0.0 copy-start.3
  8.0 0.0 copy-start
  8.0 17.7 %while.22 = (s32[]{:T(128)}, f32[2048,128]{1,0:T(8,128)S(1)}, s32[4,2048]{1,0:T(4,128)S(1)}, bf16[4,2048,128]{2,1,0:T(8,128)(2,1)}, s32[]{:T(128)}, /*index=5*/s32[]{:T(128)}) while((s32[]{:T(128)}, f32[2048,128]{1,0:T(8,128)S(1)}, s32[4,2048]{1,0:T(4,128)S(1)}, bf16[4,2048,128]{2,1,0:T(8,128)(2,1)}, s32[]{:T(128)}, ...), condition=%wide.region_1.2_spmd.clone, body=%wide.region_0.1_spmd.clone.sunk | while | flops 1078460416 | bytes 2646611 | solution.py:23
  8.1 4.4 %fusion.21 = f32[2048,128]{1,0:T(8,128)S(1)} fusion(s32[2048]{0:T(1024)S(1)} %bitcast.25, f32[2048,128]{1,0:T(8,128)S(1)} %get-tuple-element.165, bf16[4,2048,128]{2,1,0:T(8,128)(2,1)} %get-tuple-element.173, s32[]{:T(128)} %get-tuple-element.164, pred[]{:T(512)S(6)} %compare.6), kind=kOutput, calls=%fused_computation.5.clone.1 | convolution fusion | flops 1078460416 | bytes 2630145 | tf_op jit(solution)/shard_map/while/body/eval_jaxpr/dot_general | solution.py:20
  12.6 4.4 %fusion.21 = f32[2048,128]{1,0:T(8,128)S(1)} fusion(s32[2048]{0:T(1024)S(1)} %bitcast.25, f32[2048,128]{1,0:T(8,128)S(1)} %get-tuple-element.165, bf16[4,2048,128]{2,1,0:T(8,128)(2,1)} %get-tuple-element.173, s32[]{:T(128)} %get-tuple-element.164, pred[]{:T(512)S(6)} %compare.6), kind=kOutput, calls=%fused_computation.5.clone.1 | convolution fusion | flops 1078460416 | bytes 2630145 | tf_op jit(solution)/shard_map/while/body/eval_jaxpr/dot_general | solution.py:20
  17.0 4.4 %fusion.21 = f32[2048,128]{1,0:T(8,128)S(1)} fusion(s32[2048]{0:T(1024)S(1)} %bitcast.25, f32[2048,128]{1,0:T(8,128)S(1)} %get-tuple-element.165, bf16[4,2048,128]{2,1,0:T(8,128)(2,1)} %get-tuple-element.173, s32[]{:T(128)} %get-tuple-element.164, pred[]{:T(512)S(6)} %compare.6), kind=kOutput, calls=%fused_computation.5.clone.1 | convolution fusion | flops 1078460416 | bytes 2630145 | tf_op jit(solution)/shard_map/while/body/eval_jaxpr/dot_general | solution.py:20
  21.4 4.4 %fusion.21 = f32[2048,128]{1,0:T(8,128)S(1)} fusion(s32[2048]{0:T(1024)S(1)} %bitcast.25, f32[2048,128]{1,0:T(8,128)S(1)} %get-tuple-element.165, bf16[4,2048,128]{2,1,0:T(8,128)(2,1)} %get-tuple-element.173, s32[]{:T(128)} %get-tuple-element.164, pred[]{:T(512)S(6)} %compare.6), kind=kOutput, calls=%fused_computation.5.clone.1 | convolution fusion | flops 1078460416 | bytes 2630145 | tf_op jit(solution)/shard_map/while/body/eval_jaxpr/dot_general | solution.py:20
  25.7 0.0 copy-start.1
  25.8 1.0 copy-done.1
  26.7 0.0 reduce-scatter.2.cloned.1.call-update
  26.7 0.0 copy-done.2
  26.8 0.6 all_to_all.9
  27.4 7.3 %all-to-all-start = ((s32[8,1,512]{2,1,0:T(1,128)}), s32[8,1,512]{2,1,0:T(1,128)S(1)}, u32[]{:S(2)}, u32[]{:S(2)}) async-start(s32[8,1,512]{2,1,0:T(1,128)} %all_to_all.9), calls=%async_computation.1 | async-start | bytes 32768 | tf_op jit(solution)/shard_map/all_to_all | solution.py:48
  34.7 0.0 copy-done.3
  34.7 0.1 iota_compare_fusion.8
  34.8 0.0 copy-done
  34.8 1.5 bitcast_select_fusion
  36.2 5.1 %all-to-all-done = s32[8,1,512]{2,1,0:T(1,128)S(1)} async-done(((s32[8,1,512]{2,1,0:T(1,128)}), s32[8,1,512]{2,1,0:T(1,128)S(1)}, u32[]{:S(2)}, u32[]{:S(2)}) %all-to-all-start) | async-done | bytes 16416 | tf_op jit(solution)/shard_map/all_to_all | solution.py:48
  41.3 3.6 %all-to-all-start.1 = ((bf16[8,512,128]{2,1,0:T(8,128)(2,1)}), bf16[8,512,128]{2,1,0:T(8,128)(2,1)S(1)}, u32[]{:S(2)}, u32[]{:S(2)}) async-start(bf16[8,512,128]{2,1,0:T(8,128)(2,1)} %bitcast_select_fusion), calls=%async_computation.2 | async-start | bytes 2097152 | tf_op jit(solution)/shard_map/all_to_all | solution.py:47
  44.9 0.0 all-reduce.2.cloned.1.call-start
  44.9 56.6 %reduce-scatter.2.cloned.1.call-done = f32[256,128]{1,0:T(8,128)} async-done(((f32[2048,128]{1,0:T(8,128)}), f32[256,128]{1,0:T(8,128)}) %reduce-scatter.2.cloned.1.call-update) | async-done | bytes 131088 | tf_op jit(solution)/shard_map/reduce_scatter | solution.py:32
  101.6 0.0 all-reduce.2.cloned.1.call-update
  101.6 0.0 all-gather.2.cloned.1.call-start
  101.6 32.9 %all-reduce.2.cloned.1.call-done = f32[256,128]{1,0:T(8,128)} async-done(((f32[256,128]{1,0:T(8,128)}), f32[256,128]{1,0:T(8,128)}) %all-reduce.2.cloned.1.call-update) | async-done | bytes 131088 | tf_op jit(solution)/shard_map/psum | solution.py:33
  134.6 0.0 all-gather.2.cloned.1.call-update
  134.7 0.0 all-to-all-done.1
  134.7 7.3 %while.23 = (s32[]{:T(128)}, f32[2048,128]{1,0:T(8,128)S(1)}, s32[4,1024]{1,0:T(4,128)S(1)}, bf16[4,1024,128]{2,1,0:T(8,128)(2,1)S(1)}, s32[]{:T(128)}, /*index=5*/s32[]{:T(128)}) while((s32[]{:T(128)}, f32[2048,128]{1,0:T(8,128)S(1)}, s32[4,1024]{1,0:T(4,128)S(1)}, bf16[4,1024,128]{2,1,0:T(8,128)(2,1)S(1)}, s32[]{:T(128)}, ...), condition=%wide.region_5.6_spmd.clone, body=%wide.region_4.5_spmd.clone.sunk | while | flops 539492352 | bytes 2371671 | solution.py:23
  134.7 1.8 fusion.23
  136.5 1.8 fusion.23
  138.4 1.8 fusion.23
  140.2 1.8 fusion.23
  142.0 0.0 copy-start.4
  142.0 35.0 %all-gather.2.cloned.1.call-done = f32[2048,128]{1,0:T(8,128)} async-done(((f32[256,128]{1,0:T(8,128)}), f32[2048,128]{1,0:T(8,128)}) %all-gather.2.cloned.1.call-update) | async-done | bytes 1048592 | tf_op jit(solution)/shard_map/all_gather | solution.py:34
  177.0 2.3 %broadcast_multiply_fusion = f32[2048,128]{1,0:T(8,128)} fusion(f32[2048,128]{1,0:T(8,128)} %all-gather.2.cloned.1.call-done), kind=kLoop, calls=%fused_computation.19 | loop fusion | flops 262144 | bytes 2097152 | tf_op jit(solution)/shard_map/mul | solution.py:35
  179.3 0.0 copy-done.4
  (12 shorter events, 0.1 us)
Async XLA Ops:
  7.2 94.4 %reduce-scatter.2.cloned.1.call-start = ((), (), s32[]{:S(2)}) async-start(), calls=%async_computation.3 | async-start | bytes 1179648 | tf_op jit(solution)/shard_map/reduce_scatter | solution.py:32
  8.0 18.8 %copy-start.2 = (s32[1,1,8,512]{3,2,1,0:T(8,128)S(1)}, s32[1,1,8,512]{3,2,1,0:T(8,128)}, u32[]{:S(2)}) copy-start(s32[1,1,8,512]{3,2,1,0:T(8,128)} %param.12) | copy-start | bytes 49156
  8.0 26.7 %copy-start.3 = (s32[1,1,8]{2,1,0:T(1,128)S(1)}, s32[1,1,8]{2,1,0:T(1,128)}, u32[]{:S(2)}) copy-start(s32[1,1,8]{2,1,0:T(1,128)} %param.13) | copy-start | bytes 100
  8.0 26.7 %copy-start = (bf16[1,1,8,512,128]{4,3,2,1,0:T(8,128)(2,1)S(1)}, bf16[1,1,8,512,128]{4,3,2,1,0:T(8,128)(2,1)}, u32[]{:S(2)}) copy-start(bf16[1,1,8,512,128]{4,3,2,1,0:T(8,128)(2,1)} %param.11) | copy-start | bytes 3145732
  25.7 1.0 copy-start.1
  27.4 13.9 %all-to-all-start = ((s32[8,1,512]{2,1,0:T(1,128)}), s32[8,1,512]{2,1,0:T(1,128)S(1)}, u32[]{:S(2)}, u32[]{:S(2)}) async-start(s32[8,1,512]{2,1,0:T(1,128)} %all_to_all.9), calls=%async_computation.1 | async-start | bytes 32768 | tf_op jit(solution)/shard_map/all_to_all | solution.py:48
  41.3 93.4 %all-to-all-start.1 = ((bf16[8,512,128]{2,1,0:T(8,128)(2,1)}), bf16[8,512,128]{2,1,0:T(8,128)(2,1)S(1)}, u32[]{:S(2)}, u32[]{:S(2)}) async-start(bf16[8,512,128]{2,1,0:T(8,128)(2,1)} %bitcast_select_fusion), calls=%async_computation.2 | async-start | bytes 2097152 | tf_op jit(solution)/shard_map/all_to_all | solution.py:47
  44.9 89.7 %all-reduce.2.cloned.1.call-start = ((), (), s32[]{:S(2)}) async-start(), calls=%async_computation.4 | async-start | bytes 262144 | tf_op jit(solution)/shard_map/psum | solution.py:33
  101.6 75.4 %all-gather.2.cloned.1.call-start = ((), (), s32[]{:S(2)}) async-start(), calls=%async_computation.5 | async-start | bytes 1179648 | tf_op jit(solution)/shard_map/all_gather | solution.py:34
  142.0 37.3 %copy-start.4 = (f32[2048,128]{1,0:T(8,128)}, f32[2048,128]{1,0:T(8,128)S(1)}, u32[]{:S(2)}) copy-start(f32[2048,128]{1,0:T(8,128)S(1)} %get-tuple-element.57) | copy-start | bytes 3145732
Sparse Core Ops, SparseCore 0:
  26.9 74.6 reduce-scatter.1
  103.9 30.6 all-reduce.1
  136.7 40.2 all-gather.1
where the time goes:
time: 186 us
  waiting for transfers between devices  130 us (70%)
  matrix products  24.7 us (13%)
  between operations  13.9 us (7%)
  starting transfers between devices  11 us (6%)
  other arithmetic  3.89 us (2%)
  local copies, waits for them, and re-layouts  2.47 us (1%)
    reduce_scatter x1, waiting for transfers between devices, hot_part(): shared = lax.psum_scatter(local_sum, 'gy', scatter_dimension=0, tiled=True)  56.6 us
    all_gather x1, waiting for transfers between devices, hot_part(): total = lax.all_gather(shared, 'gy', axis=0, tiled=True)  35 us
    psum x1, waiting for transfers between devices, hot_part(): shared = lax.psum(shared, 'gx')  32.9 us
    dot_general x8, matrix products, add_block(): jnp.dot(selector, data_here, preferred_element_type=jnp.float32)  24.7 us
    all_to_all x1, starting transfers between devices, cold_part(): lax.all_to_all(slots_here, 'gy', split_axis=0, concat_axis=0, tiled=True)  7.31 us
    all_to_all x1, waiting for transfers between devices, cold_part(): lax.all_to_all(slots_here, 'gy', split_axis=0, concat_axis=0, tiled=True)  5.07 us
  transfers between devices with their start and end apart: 5, of which 4 were waited for; matrix products, arithmetic and copies ran while one was open for 5% of the time, Pallas kernels for 0%

commit v1 on v0

--- a/solution.py
+++ b/solution.py
@@ -6,6 +6,10 @@
 
 HOT = 2048
 OWN_ROWS = 2048
+
+
+def chains_state(load):
+    return jnp.sum(jax.lax.all_gather(load, "gx"), 0)
 
 
 def onehot_sum(row_ids, row_data, table_size, block_rows):
@@ -30,7 +34,7 @@
     local_sum = onehot_sum(hot_ids, hot_grads, hot_rows, block_rows)
     factor = (hot_rows / (hot_ids.shape[0] * lax.axis_size("gx") * lax.axis_size("gy"))) ** 0.5
     shared = lax.psum_scatter(local_sum, "gy", scatter_dimension=0, tiled=True)
-    shared = lax.psum(shared, "gx")
+    shared = chains_state(shared)
     total = lax.all_gather(shared, "gy", axis=0, tiled=True)
     return total * factor
 

time: 186 us -> 158 us (0.85)
  waiting for transfers between devices: 130 us -> 93 us
  blocking collectives: 0 us -> 7.33 us
    psum x1 -> x0, waiting for transfers between devices: 32.9 us -> none  [hot_part(): shared = lax.psum(shared, 'gx')]
    all_gather x0 -> x1, blocking collectives: none -> 7.33 us  [chains_state(): return jnp.sum(jax.lax.all_gather(load, 'gx'), 0)]
    all_gather x1, waiting for transfers between devices: 35 us -> 31.3 us  [hot_part(): total = lax.all_gather(shared, 'gy', axis=0, tiled=True)]
  transfers between devices with their start and end apart: 5 -> 4, of which waited for: 4 -> 3; matrix products, arithmetic and copies ran while one was open for 5% -> 6% of each run, Pallas kernels for 0% -> 0%
where the time goes in v1:
time: 158 us; the launch traced here: 157 us
  waiting for transfers between devices  93 us (59%)
  matrix products  24.7 us (16%)
  between operations  14.2 us (9%)
  starting transfers between devices  10.9 us (7%)
  blocking collectives  7.33 us (5%)
  other arithmetic  4.57 us (3%)
  local copies, waits for them, and re-layouts  2.47 us (2%)
    reduce_scatter x1, waiting for transfers between devices, hot_part(): shared = lax.psum_scatter(local_sum, 'gy', scatter_dimension=0, tiled=True)  56.6 us
    all_gather x1, waiting for transfers between devices, hot_part(): total = lax.all_gather(shared, 'gy', axis=0, tiled=True)  31.3 us
    dot_general x8, matrix products, add_block(): jnp.dot(selector, data_here, preferred_element_type=jnp.float32)  24.7 us
    all_gather x1, blocking collectives, chains_state(): return jnp.sum(jax.lax.all_gather(load, 'gx'), 0)  7.33 us
    all_to_all x1, starting transfers between devices, cold_part(): lax.all_to_all(slots_here, 'gy', split_axis=0, concat_axis=0, tiled=True)  7.31 us
    all_to_all x1, waiting for transfers between devices, cold_part(): lax.all_to_all(slots_here, 'gy', split_axis=0, concat_axis=0, tiled=True)  5.07 us
    all_to_all x1, starting transfers between devices, cold_part(): lax.all_to_all(payload, 'gy', split_axis=0, concat_axis=0, tiled=True)  3.56 us
  transfers between devices with their start and end apart: 4, of which 3 were waited for; matrix products, arithmetic and copies ran while one was open for 6% of the time, Pallas kernels for 0%

profile of v1, /device:TPU:0, one launch (start us, length us, event | category | flops | bytes accessed | tf_op | source)
XLA Modules:
  0.0 157.4 jit_solution(13209905520132617439)
XLA Ops:
  7.2 0.0 reduce-scatter.2.cloned.1.call-start
  7.2 0.8 reshape.43
  8.0 0.0 copy-start.2
  8.0 0.0 copy-start.3
  8.0 0.0 copy-start
  8.0 17.7 %while.22 = (s32[]{:T(128)}, f32[2048,128]{1,0:T(8,128)S(1)}, s32[4,2048]{1,0:T(4,128)S(1)}, bf16[4,2048,128]{2,1,0:T(8,128)(2,1)}, s32[]{:T(128)}, /*index=5*/s32[]{:T(128)}) while((s32[]{:T(128)}, f32[2048,128]{1,0:T(8,128)S(1)}, s32[4,2048]{1,0:T(4,128)S(1)}, bf16[4,2048,128]{2,1,0:T(8,128)(2,1)}, s32[]{:T(128)}, ...), condition=%wide.region_1.2_spmd.clone, body=%wide.region_0.1_spmd.clone.sunk | while | flops 1078460416 | bytes 2646111 | solution.py:27
  8.1 4.4 %fusion.21 = f32[2048,128]{1,0:T(8,128)S(1)} fusion(s32[2048]{0:T(1024)S(1)} %bitcast.27, f32[2048,128]{1,0:T(8,128)S(1)} %get-tuple-element.165, bf16[4,2048,128]{2,1,0:T(8,128)(2,1)} %get-tuple-element.173, s32[]{:T(128)S(6)} %copy.9, pred[]{:T(512)S(6)} %compare.6), kind=kOutput, calls=%fused_computation.5.clone.1 | convolution fusion | flops 1078460416 | bytes 2629637 | tf_op jit(solution)/shard_map/while/body/eval_jaxpr/dot_general | solution.py:24
  12.6 4.4 %fusion.21 = f32[2048,128]{1,0:T(8,128)S(1)} fusion(s32[2048]{0:T(1024)S(1)} %bitcast.27, f32[2048,128]{1,0:T(8,128)S(1)} %get-tuple-element.165, bf16[4,2048,128]{2,1,0:T(8,128)(2,1)} %get-tuple-element.173, s32[]{:T(128)S(6)} %copy.9, pred[]{:T(512)S(6)} %compare.6), kind=kOutput, calls=%fused_computation.5.clone.1 | convolution fusion | flops 1078460416 | bytes 2629637 | tf_op jit(solution)/shard_map/while/body/eval_jaxpr/dot_general | solution.py:24
  17.0 4.4 %fusion.21 = f32[2048,128]{1,0:T(8,128)S(1)} fusion(s32[2048]{0:T(1024)S(1)} %bitcast.27, f32[2048,128]{1,0:T(8,128)S(1)} %get-tuple-element.165, bf16[4,2048,128]{2,1,0:T(8,128)(2,1)} %get-tuple-element.173, s32[]{:T(128)S(6)} %copy.9, pred[]{:T(512)S(6)} %compare.6), kind=kOutput, calls=%fused_computation.5.clone.1 | convolution fusion | flops 1078460416 | bytes 2629637 | tf_op jit(solution)/shard_map/while/body/eval_jaxpr/dot_general | solution.py:24
  21.4 4.4 %fusion.21 = f32[2048,128]{1,0:T(8,128)S(1)} fusion(s32[2048]{0:T(1024)S(1)} %bitcast.27, f32[2048,128]{1,0:T(8,128)S(1)} %get-tuple-element.165, bf16[4,2048,128]{2,1,0:T(8,128)(2,1)} %get-tuple-element.173, s32[]{:T(128)S(6)} %copy.9, pred[]{:T(512)S(6)} %compare.6), kind=kOutput, calls=%fused_computation.5.clone.1 | convolution fusion | flops 1078460416 | bytes 2629637 | tf_op jit(solution)/shard_map/while/body/eval_jaxpr/dot_general | solution.py:24
  25.8 0.0 copy-start.1
  25.8 1.0 copy-done.1
  26.7 0.0 reduce-scatter.2.cloned.1.call-update
  26.8 0.0 copy-done.2
  26.8 0.6 all_to_all.9
  27.4 7.3 %all-to-all-start = ((s32[8,1,512]{2,1,0:T(1,128)}), s32[8,1,512]{2,1,0:T(1,128)S(1)}, u32[]{:S(2)}, u32[]{:S(2)}) async-start(s32[8,1,512]{2,1,0:T(1,128)} %all_to_all.9), calls=%async_computation.1 | async-start | bytes 32768 | tf_op jit(solution)/shard_map/all_to_all | solution.py:52
  34.7 0.0 copy-done.3
  34.7 0.1 iota_compare_fusion.8
  34.8 0.0 copy-done
  34.8 1.5 bitcast_select_fusion
  36.2 5.1 %all-to-all-done = s32[8,1,512]{2,1,0:T(1,128)S(1)} async-done(((s32[8,1,512]{2,1,0:T(1,128)}), s32[8,1,512]{2,1,0:T(1,128)S(1)}, u32[]{:S(2)}, u32[]{:S(2)}) %all-to-all-start) | async-done | bytes 16416 | tf_op jit(solution)/shard_map/all_to_all | solution.py:52
  41.3 3.6 %all-to-all-start.1 = ((bf16[8,512,128]{2,1,0:T(8,128)(2,1)}), bf16[8,512,128]{2,1,0:T(8,128)(2,1)S(1)}, u32[]{:S(2)}, u32[]{:S(2)}) async-start(bf16[8,512,128]{2,1,0:T(8,128)(2,1)} %bitcast_select_fusion), calls=%async_computation.2 | async-start | bytes 2097152 | tf_op jit(solution)/shard_map/all_to_all | solution.py:51
  44.9 0.0 all-gather.3.cloned.1.call-start
  44.9 56.6 %reduce-scatter.2.cloned.1.call-done = f32[256,128]{1,0:T(8,128)} async-done(((f32[2048,128]{1,0:T(8,128)}), f32[256,128]{1,0:T(8,128)}) %reduce-scatter.2.cloned.1.call-update) | async-done | bytes 131088 | tf_op jit(solution)/shard_map/reduce_scatter | solution.py:36
  101.6 7.3 %all-gather = f32[1024,128]{1,0:T(8,128)S(1)} all-gather(f32[256,128]{1,0:T(8,128)} %reduce-scatter.2.cloned.1.call-done), channel_id=2, replica_groups=mesh['gx'=4,'gy'=8] {'gx'}, dimensions={0}, use_global_device_ids=true | all-gather | bytes 655360 | tf_op jit(solution)/shard_map/all_gather | solution.py:12
  108.9 0.7 reduce_sum.9
  109.6 0.0 all-gather.3.cloned.1.call-update
  109.7 0.0 all-to-all-done.1
  109.7 7.3 %while.23 = (s32[]{:T(128)}, f32[2048,128]{1,0:T(8,128)S(1)}, s32[4,1024]{1,0:T(4,128)S(1)}, bf16[4,1024,128]{2,1,0:T(8,128)(2,1)S(1)}, s32[]{:T(128)}, /*index=5*/s32[]{:T(128)}) while((s32[]{:T(128)}, f32[2048,128]{1,0:T(8,128)S(1)}, s32[4,1024]{1,0:T(4,128)S(1)}, bf16[4,1024,128]{2,1,0:T(8,128)(2,1)S(1)}, s32[]{:T(128)}, ...), condition=%wide.region_5.6_spmd.clone, body=%wide.region_4.5_spmd.clone.sunk | while | flops 539492352 | bytes 2371679 | solution.py:27
  109.7 1.8 %fusion.23 = f32[2048,128]{1,0:T(8,128)S(1)} fusion(s32[1024]{0:T(1024)S(1)} %bitcast.28, f32[2048,128]{1,0:T(8,128)S(1)} %get-tuple-element.183, pred[]{:T(512)S(6)} %compare.7, bf16[4,1024,128]{2,1,0:T(8,128)(2,1)S(1)} %get-tuple-element.191, s32[]{:T(128)S(6)} %copy.15), kind=kOutput, calls=%fused_computation.13.clone.1 | convolution fusion | flops 539492352 | bytes 2363397 | tf_op jit(solution)/shard_map/while/body/eval_jaxpr/dot_general | solution.py:24
  111.5 1.8 %fusion.23 = f32[2048,128]{1,0:T(8,128)S(1)} fusion(s32[1024]{0:T(1024)S(1)} %bitcast.28, f32[2048,128]{1,0:T(8,128)S(1)} %get-tuple-element.183, pred[]{:T(512)S(6)} %compare.7, bf16[4,1024,128]{2,1,0:T(8,128)(2,1)S(1)} %get-tuple-element.191, s32[]{:T(128)S(6)} %copy.15), kind=kOutput, calls=%fused_computation.13.clone.1 | convolution fusion | flops 539492352 | bytes 2363397 | tf_op jit(solution)/shard_map/while/body/eval_jaxpr/dot_general | solution.py:24
  113.4 1.8 %fusion.23 = f32[2048,128]{1,0:T(8,128)S(1)} fusion(s32[1024]{0:T(1024)S(1)} %bitcast.28, f32[2048,128]{1,0:T(8,128)S(1)} %get-tuple-element.183, pred[]{:T(512)S(6)} %compare.7, bf16[4,1024,128]{2,1,0:T(8,128)(2,1)S(1)} %get-tuple-element.191, s32[]{:T(128)S(6)} %copy.15), kind=kOutput, calls=%fused_computation.13.clone.1 | convolution fusion | flops 539492352 | bytes 2363397 | tf_op jit(solution)/shard_map/while/body/eval_jaxpr/dot_general | solution.py:24
  115.2 1.8 %fusion.23 = f32[2048,128]{1,0:T(8,128)S(1)} fusion(s32[1024]{0:T(1024)S(1)} %bitcast.28, f32[2048,128]{1,0:T(8,128)S(1)} %get-tuple-element.183, pred[]{:T(512)S(6)} %compare.7, bf16[4,1024,128]{2,1,0:T(8,128)(2,1)S(1)} %get-tuple-element.191, s32[]{:T(128)S(6)} %copy.15), kind=kOutput, calls=%fused_computation.13.clone.1 | convolution fusion | flops 539492352 | bytes 2363397 | tf_op jit(solution)/shard_map/while/body/eval_jaxpr/dot_general | solution.py:24
  117.0 0.0 copy-start.4
  117.0 31.3 %all-gather.3.cloned.1.call-done = f32[2048,128]{1,0:T(8,128)} async-done(((f32[256,128]{1,0:T(8,128)}), f32[2048,128]{1,0:T(8,128)}) %all-gather.3.cloned.1.call-update) | async-done | bytes 1048592 | tf_op jit(solution)/shard_map/all_gather | solution.py:38
  148.3 2.3 %broadcast_multiply_fusion = f32[2048,128]{1,0:T(8,128)} fusion(f32[2048,128]{1,0:T(8,128)} %all-gather.3.cloned.1.call-done), kind=kLoop, calls=%fused_computation.19 | loop fusion | flops 262144 | bytes 2097152 | tf_op jit(solution)/shard_map/mul | solution.py:39
  150.6 0.0 copy-done.4
  (12 shorter events, 0.1 us)
Async XLA Ops:
  7.2 94.4 %reduce-scatter.2.cloned.1.call-start = ((), (), s32[]{:S(2)}) async-start(), calls=%async_computation.3 | async-start | bytes 1179648 | tf_op jit(solution)/shard_map/reduce_scatter | solution.py:36
  8.0 18.8 %copy-start.2 = (s32[1,1,8,512]{3,2,1,0:T(8,128)S(1)}, s32[1,1,8,512]{3,2,1,0:T(8,128)}, u32[]{:S(2)}) copy-start(s32[1,1,8,512]{3,2,1,0:T(8,128)} %param.12) | copy-start | bytes 49156
  8.0 26.7 %copy-start.3 = (s32[1,1,8]{2,1,0:T(1,128)S(1)}, s32[1,1,8]{2,1,0:T(1,128)}, u32[]{:S(2)}) copy-start(s32[1,1,8]{2,1,0:T(1,128)} %param.13) | copy-start | bytes 100
  8.0 26.7 %copy-start = (bf16[1,1,8,512,128]{4,3,2,1,0:T(8,128)(2,1)S(1)}, bf16[1,1,8,512,128]{4,3,2,1,0:T(8,128)(2,1)}, u32[]{:S(2)}) copy-start(bf16[1,1,8,512,128]{4,3,2,1,0:T(8,128)(2,1)} %param.11) | copy-start | bytes 3145732
  25.8 1.0 copy-start.1
  27.4 13.9 %all-to-all-start = ((s32[8,1,512]{2,1,0:T(1,128)}), s32[8,1,512]{2,1,0:T(1,128)S(1)}, u32[]{:S(2)}, u32[]{:S(2)}) async-start(s32[8,1,512]{2,1,0:T(1,128)} %all_to_all.9), calls=%async_computation.1 | async-start | bytes 32768 | tf_op jit(solution)/shard_map/all_to_all | solution.py:52
  41.3 68.4 %all-to-all-start.1 = ((bf16[8,512,128]{2,1,0:T(8,128)(2,1)}), bf16[8,512,128]{2,1,0:T(8,128)(2,1)S(1)}, u32[]{:S(2)}, u32[]{:S(2)}) async-start(bf16[8,512,128]{2,1,0:T(8,128)(2,1)} %bitcast_select_fusion), calls=%async_computation.2 | async-start | bytes 2097152 | tf_op jit(solution)/shard_map/all_to_all | solution.py:51
  44.9 103.4 %all-gather.3.cloned.1.call-start = ((), (), s32[]{:S(2)}) async-start(), calls=%async_computation.4 | async-start | bytes 1179648 | tf_op jit(solution)/shard_map/all_gather | solution.py:38
  117.0 33.6 %copy-start.4 = (f32[2048,128]{1,0:T(8,128)}, f32[2048,128]{1,0:T(8,128)S(1)}, u32[]{:S(2)}) copy-start(f32[2048,128]{1,0:T(8,128)S(1)} %get-tuple-element.57) | copy-start | bytes 3145732
Sparse Core Ops, SparseCore 0:
  26.9 74.6 reduce-scatter.1
  109.7 38.5 all-gather.2
